TPU v7x, 256 devices: a 8x8x2 block of a 8x8x16 slice. The times are simulated.
256 devices in a mesh: groups: 2 (over z), expert: 16 (over x, core), cuts: 8 (over y).
Axes of the slice: x: 8, y: 8, z: 2, core: 2. Of those that a mesh axis runs over, the one named last changes fastest.
The devices are a block of a 8x8x16 slice.
Arguments:
- tokens: bfloat16 [16384, 2048], P(('groups', 'expert')), parts along dimension 0, may hold values from -6 to 6
- route: int32 [16384, 1], P(('groups', 'expert')), parts along dimension 0, may hold values from 0 to 15; in each aligned block of 512 rows (0 to 511, 512 to 1023, ...) at most 48 rows name the same one
- gate_prob: float32 [16384], P(('groups', 'expert')), parts along dimension 0, may hold values from 0.2 to 1
- norm_gain: float32 [2048], replicated, may hold values from 0.5 to 1.5
- dense_in: bfloat16 [2048, 8192], P('expert', 'cuts'), may hold values from -0.125 to 0.125
- dense_out: bfloat16 [8192, 2048], P('cuts', 'expert'), may hold values from -0.0625 to 0.0625
- expert_in: bfloat16 [16, 2048, 8192], P('expert', None, 'cuts'), may hold values from -0.125 to 0.125
- expert_out: bfloat16 [16, 8192, 2048], P('expert', 'cuts'), may hold values from -0.0625 to 0.0625
Outputs:
- layer_out: bfloat16 [16384, 2048], P(('groups', 'expert'), 'cuts'), parts along dimension 0
There are 2 independent parts, one for each index of `groups`. A program takes and returns all parts, laid end to end along the dimension named above; an argument that names none is the same for every part. Nothing has to cross between parts.
Inputs may be any that keep to these rules, and one draw needn't show every extreme that they name: `route`: within the rows of one device (aligned blocks of 512 rows) no expert is named by more than 48 rows; in some blocks one expert is named by exactly 48 rows.
All inputs are finite; a program needn't handle non-finite values.
Results may differ from a plain program's by a relative error of at most 0.0095.
Values may be sent and summed in bfloat16 or wider, within the bound.
A program may use at most 64 MiB of HBM per device.

v0:
```python
import jax
import jax.numpy as jnp
from jax import lax
from jax.sharding import PartitionSpec as P


def normalize(tokens, norm_gain):
    widened = tokens.astype(jnp.float32)
    meansq = jnp.mean(widened * widened, axis=-1, keepdims=True)
    return (widened * lax.rsqrt(meansq + 1e-06) * norm_gain).astype(jnp.bfloat16)


def residual_mlp(normed, dense_in, dense_out):
    before_act = jnp.dot(
        normed,
        lax.all_gather(dense_in, "expert", axis=0, tiled=True),
        preferred_element_type=jnp.float32,
    )
    dense_act = jax.nn.gelu(before_act).astype(jnp.bfloat16)
    partial_out = jnp.dot(
        dense_act,
        lax.all_gather(dense_out, "expert", axis=1, tiled=True),
        preferred_element_type=jnp.float32,
    )
    return lax.psum_scatter(
        partial_out.astype(jnp.bfloat16), "cuts", scatter_dimension=1, tiled=True
    ).astype(jnp.float32)


def local(tokens, route, gate_prob, norm_gain, dense_in, dense_out, expert_in, expert_out):
    experts = lax.axis_size("expert")
    slices = lax.axis_size("cuts")
    tok_rows, width = tokens.shape
    share = width // slices
    capacity = max(2, 3 * tok_rows // (2 * experts))
    normed = normalize(tokens, norm_gain)
    dense = residual_mlp(normed, dense_in, dense_out)
    picked = route[:, 0]
    labels = jnp.arange(experts, dtype=jnp.int32)
    one_hot = (picked[:, None] == labels[None, :]).astype(jnp.int32)
    before = jnp.cumsum(one_hot, axis=0) - one_hot
    position = jnp.sum(before * one_hot, axis=-1)
    target = picked * capacity + position
    outgoing = jnp.zeros((experts * capacity, width), jnp.bfloat16).at[target].set(normed)
    outgoing = outgoing.reshape(experts, capacity, width)
    weight_in = expert_in[0]
    weight_out = expert_out[0]
    arrived = lax.all_to_all(outgoing, "expert", split_axis=0, concat_axis=0, tiled=True)
    sources = arrived.shape[0]
    count = arrived.shape[1]
    flat_rows = arrived.reshape(sources * count, width)
    inner = jax.nn.gelu(jnp.dot(flat_rows, weight_in, preferred_element_type=jnp.float32)).astype(
        jnp.bfloat16
    )
    partial_res = jnp.dot(inner, weight_out, preferred_element_type=jnp.float32).reshape(
        sources, count, width
    )
    cut_index = lax.axis_index("cuts")
    own_share = lax.psum_scatter(
        partial_res.astype(jnp.bfloat16), "cuts", scatter_dimension=2, tiled=True
    )
    returned = lax.all_to_all(own_share, "expert", split_axis=0, concat_axis=0, tiled=True)
    expert_res = returned.reshape(experts * capacity, share)[target].astype(jnp.float32)
    own_tokens = lax.dynamic_slice_in_dim(tokens, cut_index * share, share, 1).astype(jnp.float32)
    layer_out = own_tokens + dense + gate_prob[:, None] * expert_res
    return layer_out.astype(jnp.bfloat16)


def solution(mesh):
    return jax.shard_map(
        local,
        mesh=mesh,
        in_specs=(
            P(("groups", "expert"), None),
            P(("groups", "expert"), None),
            P(("groups", "expert")),
            P(),
            P("expert", "cuts"),
            P("cuts", "expert"),
            P("expert", None, "cuts"),
            P("expert", "cuts", None),
        ),
        out_specs=P(("groups", "expert"), "cuts"),
        check_vma=False,
    )
```

profile of v0, /device:TPU:513, one launch (start us, length us, event | category | flops | bytes accessed | tf_op | source)
XLA Modules:
  0.0 239.2 jit_solution(17498431186628819330)
XLA Ops:
  7.4 0.0 all-gather.3.cloned.1.call-start
  7.4 0.7 all-gather.3.cloned.1.call-update
  8.2 0.1 all-gather.5.cloned.1.call-start
  8.2 0.7 all-gather.5.cloned.1.call-update
  9.0 0.1 reduce-scatter.5.cloned.1.call-start
  9.0 2.1 fusion
  11.1 0.7 fusion.45
  11.8 1.1 reduce-window.6
  13.0 0.2 slice_reduce_fusion
  13.2 0.8 fusion.44
  14.0 0.7 compare_select_fusion
  14.7 5.9 %scatter_custom_fusion = bf16[768,2048]{1,0:T(8,128)(2,1)S(1)} fusion(s32[512]{0:T(512)S(1)} %bitcast.48, bf16[]{:T(256)} %constant.9.clone.1, bf16[512,2048]{1,0:T(8,128)(2,1)} %param.8, f32[2048]{0:T(1024)} %param.11, f32[512]{0:T(512)S(1)} %add_rsqrt_fusion), kind=kCustom, calls=%fused_computation.31 | custom fusion | flops 4194304 | bytes 5253122 | tf_op jit(solution)/shard_map/scatter | solution.py:44
  20.5 0.0 copy-start.3
  20.6 112.0 %all_to_all.10 = bf16[16,48,2048]{2,1,0:T(8,128)(2,1)S(1)} all-to-all(bf16[16,48,2048]{2,1,0:T(8,128)(2,1)S(1)} %bitcast.44), channel_id=1, replica_groups=mesh['groups'=2,'expert'=16,'cuts'=8] {'expert'}, dimensions={0} | all-to-all | bytes 6291456 | tf_op jit(solution)/shard_map/all_to_all | solution.py:48
  132.6 0.0 copy-done.3
  132.6 0.0 copy-start.4
  132.6 4.0 %fusion.17 = bf16[768,1024]{1,0:T(8,128)(2,1)S(1)} fusion(bf16[768,2048]{1,0:T(8,128)(2,1)S(1)} %bitcast.45, bf16[1,2048,1024]{2,1,0:T(8,128)(2,1)S(1)} %copy-done.3), kind=kOutput, calls=%fused_computation.20 | convolution fusion | flops 3228303360 | bytes 8912896 | tf_op jit(solution)/shard_map/dot_general | solution.py:52
  136.6 0.0 copy-done.4
  136.6 4.9 %fusion.7 = bf16[16,48,2048]{2,1,0:T(8,128)(2,1)} fusion(bf16[16,48,1024]{2,1,0:T(8,128)(2,1)S(1)} %bitcast.51, bf16[1,1024,2048]{2,1,0:T(8,128)(2,1)S(1)} %copy-done.4), kind=kOutput, calls=%fused_computation.12 | convolution fusion | flops 3222798336 | bytes 8912896 | tf_op jit(solution)/shard_map/dot_general | solution.py:55
  141.5 0.0 copy-start
  141.5 0.0 copy-start.1
  141.5 0.1 reduce-scatter.5.cloned.1.call-update
  141.5 0.2 reduce-scatter.3.cloned.1.call-start
  141.8 0.0 all-gather.3.cloned.1.call-done
  141.8 27.8 %all-gather.5.cloned.1.call-done = bf16[1024,2048]{1,0:T(8,128)(2,1)} async-done(((bf16[1024,128]{1,0:T(8,128)(2,1)}), bf16[1024,2048]{1,0:T(8,128)(2,1)}) %all-gather.5.cloned.1.call-update) | async-done | bytes 4194320 | tf_op jit(solution)/shard_map/all_gather | solution.py:22
  169.6 0.0 copy-done
  169.6 0.0 copy-done.1
  169.6 9.9 %convolution_convert_fusion = bf16[512,2048]{1,0:T(8,128)(2,1)} fusion(bf16[1024,2048]{1,0:T(8,128)(2,1)} %all-gather.5.cloned.1.call-done, bf16[2048,1024]{1,0:T(8,128)(2,1)} %all-gather.3.cloned.1.call-done, bf16[512,2048]{1,0:T(8,128)(2,1)S(1)} %copy-done, f32[2048]{0:T(1024)S(1)} %copy-done.1, f32[512]{0:T(512)S(1)} %add_rsqrt_fusion), kind=kOutput, calls=%fused_computation.22 | convolution fusion | flops 4304928768 | bytes 12593152 | tf_op jit(solution)/shard_map/dot_general | solution.py:20
  179.5 0.0 copy-start.2
  179.5 0.1 reduce-scatter.3.cloned.1.call-update
  179.5 5.9 %reduce-scatter.5.cloned.1.call-done = bf16[16,48,256]{2,1,0:T(8,128)(2,1)} async-done(((bf16[16,48,2048]{2,1,0:T(8,128)(2,1)}), bf16[16,48,256]{2,1,0:T(8,128)(2,1)}) %reduce-scatter.5.cloned.1.call-update) | async-done | bytes 393232 | tf_op jit(solution)/shard_map/reduce_scatter | solution.py:59
  185.5 9.9 %all-to-all-start.1 = ((bf16[16,48,256]{2,1,0:T(8,128)(2,1)}), bf16[16,48,256]{2,1,0:T(8,128)(2,1)S(1)}, u32[]{:S(2)}, u32[]{:S(2)}) async-start(bf16[16,48,256]{2,1,0:T(8,128)(2,1)} %reduce-scatter.5.cloned.1.call-done), calls=%async_computation.3 | async-start | bytes 786432 | tf_op jit(solution)/shard_map/all_to_all | solution.py:62
  195.4 14.5 %all-to-all-done.1 = bf16[16,48,256]{2,1,0:T(8,128)(2,1)S(1)} async-done(((bf16[16,48,256]{2,1,0:T(8,128)(2,1)}), bf16[16,48,256]{2,1,0:T(8,128)(2,1)S(1)}, u32[]{:S(2)}, u32[]{:S(2)}) %all-to-all-start.1) | async-done | bytes 393248 | tf_op jit(solution)/shard_map/all_to_all | solution.py:62
  209.9 1.9 gather_fusion
  211.8 18.1 %reduce-scatter.3.cloned.1.call-done = bf16[512,256]{1,0:T(8,128)(2,1)} async-done(((bf16[512,2048]{1,0:T(8,128)(2,1)}), bf16[512,256]{1,0:T(8,128)(2,1)}) %reduce-scatter.3.cloned.1.call-update) | async-done | bytes 262160 | tf_op jit(solution)/shard_map/reduce_scatter | solution.py:25
  230.0 0.0 copy-done.2
  230.0 1.8 add_convert_fusion
  (4 shorter events, 0.1 us)
Async XLA Ops:
  7.4 134.4 %all-gather.3.cloned.1.call-start = ((), (), s32[]{:S(2)}) async-start(), calls=%async_computation.4 | async-start | bytes 4456448 | tf_op jit(solution)/shard_map/all_gather | solution.py:16
  8.2 161.4 %all-gather.5.cloned.1.call-start = ((), (), s32[]{:S(2)}) async-start(), calls=%async_computation.5 | async-start | bytes 4456448 | tf_op jit(solution)/shard_map/all_gather | solution.py:22
  9.0 176.5 %reduce-scatter.5.cloned.1.call-start = ((), (), s32[]{:S(2)}) async-start(), calls=%async_computation.7 | async-start | bytes 3538944 | tf_op jit(solution)/shard_map/reduce_scatter | solution.py:59
  20.5 112.1 %copy-start.3 = (bf16[1,2048,1024]{2,1,0:T(8,128)(2,1)S(1)}, bf16[1,2048,1024]{2,1,0:T(8,128)(2,1)}, u32[]{:S(2)}) copy-start(bf16[1,2048,1024]{2,1,0:T(8,128)(2,1)} %param.14) | copy-start | bytes 12582916
  132.6 4.0 %copy-start.4 = (bf16[1,1024,2048]{2,1,0:T(8,128)(2,1)S(1)}, bf16[1,1024,2048]{2,1,0:T(8,128)(2,1)}, u32[]{:S(2)}) copy-start(bf16[1,1024,2048]{2,1,0:T(8,128)(2,1)} %param.15) | copy-start | bytes 12582916
  141.5 28.1 %copy-start = (bf16[512,2048]{1,0:T(8,128)(2,1)S(1)}, bf16[512,2048]{1,0:T(8,128)(2,1)}, u32[]{:S(2)}) copy-start(bf16[512,2048]{1,0:T(8,128)(2,1)} %param.8) | copy-start | bytes 6291460
  141.5 28.1 %copy-start.1 = (f32[2048]{0:T(1024)S(1)}, f32[2048]{0:T(1024)}, u32[]{:S(2)}) copy-start(f32[2048]{0:T(1024)} %param.11) | copy-start | bytes 24580
  141.5 88.5 %reduce-scatter.3.cloned.1.call-start = ((), (), s32[]{:S(2)}) async-start(), calls=%async_computation.6 | async-start | bytes 2359296 | tf_op jit(solution)/shard_map/reduce_scatter | solution.py:25
  179.5 50.5 %copy-start.2 = (f32[512]{0:T(512)S(1)}, f32[512]{0:T(512)}, u32[]{:S(2)}) copy-start(f32[512]{0:T(512)} %param.10) | copy-start | bytes 6148
  185.5 24.4 %all-to-all-start.1 = ((bf16[16,48,256]{2,1,0:T(8,128)(2,1)}), bf16[16,48,256]{2,1,0:T(8,128)(2,1)S(1)}, u32[]{:S(2)}, u32[]{:S(2)}) async-start(bf16[16,48,256]{2,1,0:T(8,128)(2,1)} %reduce-scatter.5.cloned.1.call-done), calls=%async_computation.3 | async-start | bytes 786432 | tf_op jit(solution)/shard_map/all_to_all | solution.py:62
Sparse Core Ops, SparseCore 0:
  10.0 101.7 all-gather.2
  113.6 55.8 all-gather.4
Sparse Core Ops, SparseCore 1:
  141.6 43.8 reduce-scatter.4
  187.9 42.0 reduce-scatter.2
where the time goes:
time: 243 us; the launch traced here: 239 us
  blocking collectives  112 us (46%)
  waiting for transfers between devices  67.9 us (28%)
  matrix products  18.7 us (8%)
  between operations  15 us (6%)
  other arithmetic  13.1 us (5%)
  starting transfers between devices  10.3 us (4%)
    all_to_all x1, blocking collectives, local(): lax.all_to_all(outgoing, 'expert', split_axis=0, concat_axis=0, tiled=True)  112 us
    all_gather x1, waiting for transfers between devices, residual_mlp(): lax.all_gather(dense_out, 'expert', axis=1, tiled=True)  27.8 us
    reduce_scatter x1, waiting for transfers between devices, residual_mlp(): lax.psum_scatter(partial_out.astype(jnp.bfloat16), 'cuts', scatter_dimens...  18.1 us
    all_to_all x1, waiting for transfers between devices, local(): lax.all_to_all(own_share, 'expert', split_axis=0, concat_axis=0, tiled=True)  14.5 us
    all_to_all x1, starting transfers between devices, local(): lax.all_to_all(own_share, 'expert', split_axis=0, concat_axis=0, tiled=True)  9.92 us
    dot_general x1, matrix products, residual_mlp(): jnp.dot(dense_act, lax.all_gather(dense_out, 'expert', axis=1, tiled=True...  9.92 us
    reduce_scatter x1, waiting for transfers between devices, local(): lax.psum_scatter(partial_res.astype(jnp.bfloat16), 'cuts', scatter_dimens...  5.9 us
    scatter x1, other arithmetic, local(): jnp.zeros((experts * capacity, width), jnp.bfloat16).at[target].set(normed)  5.85 us
  transfers between devices with their start and end apart: 5, of which 4 were waited for; matrix products, arithmetic and copies ran while one was open for 13% of the time, Pallas kernels for 0%

commit v1 on v0

v1 whole, which is shorter than its diff:
```python
import functools

import jax
import jax.numpy as jnp
from jax import lax
from jax.experimental import pallas as pl
from jax.experimental.pallas import tpu as pltpu
from jax.sharding import PartitionSpec as P

MESH = pl.DeviceIdType.MESH
F32 = jnp.float32
BF16 = jnp.bfloat16
CHUNKS = 4


def layer_kernel(
    dims,
    tokens_hbm,
    route_ref,
    gate_ref,
    gain_ref,
    dense_in_hbm,
    dense_out_hbm,
    expert_in_hbm,
    expert_out_hbm,
    out_ref,
    tok,
    norm,
    pick,
    outgoing,
    arrived,
    w_in,
    w_out,
    d_in,
    d_out,
    inner,
    part,
    part_in,
    result,
    returned,
    dense_act,
    dense_part,
    dense_part_in,
    load_sem,
    disp_send,
    disp_recv,
    gath_send,
    gath_recv,
    ring_send,
    ring_recv,
    sib_send,
    sib_recv,
    red_send,
    red_recv,
    ret_send,
    ret_recv,
    dred_send,
    dred_recv,
):
    n_exp, n_cut, cap, rows, width, share, hidden = dims
    n_chip = n_exp // 2
    half_x, half_y = n_chip // 2, n_cut // 2
    per_chunk = n_exp // CHUNKS
    chunk_rows = per_chunk * cap
    drows = rows // CHUNKS
    offsets = [0] + [(p + 1) // 2 if p % 2 else -(p // 2) for p in range(1, n_chip)]

    e = lax.axis_index("expert")
    c = lax.axis_index("cuts")
    x = e // 2
    core = e - 2 * x
    sibling = 2 * x + 1 - core

    def chip(offset):
        return lax.rem(x + offset + n_chip, n_chip)

    def cut(offset):
        return lax.rem(c + offset + n_cut, n_cut)

    started = []

    def send(src, dst, send_sem, recv_sem, device):
        copy = pltpu.make_async_remote_copy(
            src_ref=src,
            dst_ref=dst,
            send_sem=send_sem,
            recv_sem=recv_sem,
            device_id=device,
            device_id_type=MESH,
        )
        copy.start()
        started.append(copy)

    def arrive(dst, recv_sem, send_sem):
        pltpu.make_async_remote_copy(
            src_ref=dst,
            dst_ref=dst,
            send_sem=send_sem,
            recv_sem=recv_sem,
            device_id={"expert": sibling},
            device_id_type=MESH,
        ).wait_recv()

    loads = []
    for number, (src, dst) in enumerate(
        (
            (tokens_hbm, tok),
            (dense_in_hbm, d_in.at[x, core]),
            (dense_out_hbm, d_out.at[x, core]),
            (expert_in_hbm, w_in),
            (expert_out_hbm, w_out),
        )
    ):
        copy = pltpu.make_async_copy(src, dst, load_sem.at[number])
        copy.start()
        loads.append(copy)

    barrier = pltpu.get_barrier_semaphore()
    for step in range(1, n_exp):
        pl.semaphore_signal(
            barrier, inc=1, device_id={"expert": lax.rem(e + step, n_exp)}, device_id_type=MESH
        )
    for step in (1, -1):
        pl.semaphore_signal(barrier, inc=1, device_id={"cuts": cut(step)}, device_id_type=MESH)

    route = route_ref[...]
    hot = lax.broadcasted_iota(jnp.int32, (n_exp, rows), 0) == route
    hot = jnp.where(hot, 1.0, 0.0).astype(F32)
    earlier = lax.broadcasted_iota(jnp.int32, (rows, rows), 0) < lax.broadcasted_iota(
        jnp.int32, (rows, rows), 1
    )
    earlier = jnp.where(earlier, 1.0, 0.0).astype(BF16)
    before = jnp.dot(hot.astype(BF16), earlier, preferred_element_type=F32)
    position = jnp.sum(before * hot, axis=0, keepdims=True)
    target = route * cap + position.astype(jnp.int32)
    slots = lax.broadcasted_iota(jnp.int32, (n_exp * cap, rows), 0)
    pick[...] = jnp.where(slots == target, 1.0, 0.0).astype(BF16)

    loads[0].wait()
    block = rows // 8

    @pl.loop(0, 8)
    def _(i):
        here = pl.ds(pl.multiple_of(i * block, block), block)
        wide = tok[here, :].astype(F32)
        meansq = jnp.mean(wide * wide, axis=-1, keepdims=True)
        norm[here, :] = (wide * lax.rsqrt(meansq + 1e-06) * gain_ref[...]).astype(BF16)

    own_columns = pl.ds(pl.multiple_of(c * share, share), share)
    outgoing[...] = (
        jnp.dot(pick[...], norm[:, own_columns], preferred_element_type=F32)
        .astype(BF16)
        .reshape(n_exp, cap, share)
    )
    arrived[c, core] = outgoing[e]
    pl.semaphore_wait(barrier, n_exp + 1)

    for p in range(n_chip):
        if p == 0:
            send(
                outgoing.at[sibling],
                arrived.at[c, core],
                disp_send.at[0],
                disp_recv.at[core],
                {"expert": sibling},
            )
            continue
        for k in range(2):
            to = 2 * chip(-offsets[p]) + k
            send(
                outgoing.at[to],
                arrived.at[c, 2 * p + core],
                disp_send.at[2 * p + k],
                disp_recv.at[2 * p + core],
                {"expert": to},
            )

    weights = (d_in, d_out)

    def ring_device(way):
        return {"expert": 2 * chip(1 if way == 0 else -1) + core}

    def ring_own(w):
        own = weights[w].at[x, core]
        for way in range(2):
            send(own, own, ring_send.at[way, w, 0], ring_recv.at[way, w, 0], ring_device(way))
        send(own, own, sib_send.at[w, 0], sib_recv.at[w, 0], {"expert": sibling})

    def ring_event(w, hop):
        for way in range(2):
            if hop == half_x and w != way:
                continue
            origin = chip(-hop if way == 0 else hop)
            piece = weights[w].at[origin, core]
            arrive(piece, ring_recv.at[way, w, hop - 1], ring_send.at[way, w, 0])
            if hop < half_x - 1 or (hop == half_x - 1 and w == way):
                send(
                    piece,
                    piece,
                    ring_send.at[way, w, hop],
                    ring_recv.at[way, w, hop],
                    ring_device(way),
                )
            place = hop if way == 0 else n_chip - hop
            send(piece, piece, sib_send.at[w, place], sib_recv.at[w, place], {"expert": sibling})

    ring_events = [(w, hop) for hop in range(1, half_x + 1) for w in range(2)]

    def ring_next():
        if ring_events:
            ring_event(*ring_events.pop(0))

    loads[1].wait()
    loads[2].wait()
    ring_own(0)
    ring_own(1)

    def cut_device(way):
        return {"cuts": cut(1 if way == 0 else -1)}

    def chunk_slots(r):
        return pl.ds(r * per_chunk, per_chunk)

    def gather_event(hop, r):
        if hop == 0:
            for slot in range(r * per_chunk, (r + 1) * per_chunk):
                if slot == 0:
                    other = 1 - core
                    arrive(arrived.at[c, other], disp_recv.at[other], disp_send.at[0])
                elif slot > 1:
                    arrive(arrived.at[c, slot], disp_recv.at[slot], disp_send.at[0])
        for way in range(2):
            if hop == half_y and r % 2 != way:
                continue
            origin = cut(-hop if way == 0 else hop)
            piece = arrived.at[origin, chunk_slots(r)]
            if hop > 0:
                arrive(piece, gath_recv.at[way, hop - 1, r], gath_send.at[way, 0, 0])
            if hop < half_y - 1 or (hop == half_y - 1 and r % 2 == way):
                send(
                    piece,
                    piece,
                    gath_send.at[way, hop, r],
                    gath_recv.at[way, hop, r],
                    cut_device(way),
                )

    for hop in range(half_y):
        for r in range(CHUNKS):
            gather_event(hop, r)
            if (hop, r) in ((2, 0), (2, 3), (3, 2)):
                ring_next()

    def expert_chunk(r):
        here = chunk_slots(r)
        flat = jnp.concatenate(
            [arrived[k, here].reshape(chunk_rows, share) for k in range(n_cut)], axis=1
        )
        for n in range(2):
            columns = pl.ds(n * (hidden // 2), hidden // 2)
            inner[:, columns] = jax.nn.gelu(
                jnp.dot(flat, w_in[:, columns], preferred_element_type=F32)
            ).astype(BF16)
        for k in range(n_cut):
            part[k, here] = (
                jnp.dot(
                    inner[...], w_out[:, pl.ds(k * share, share)], preferred_element_type=F32
                )
                .astype(BF16)
                .reshape(per_chunk, cap, share)
            )

    def reduce_event(own, landed, send_sem, recv_sem, here, step, r):
        for way in range(2):
            if step == half_y and r % 2 != way:
                continue
            home = cut(step if way == 0 else -step)
            if step == half_y or (step == half_y - 1 and r % 2 != way):
                piece = own.at[home, here]
            else:
                piece = landed.at[way, step, here]
                arrive(piece, recv_sem.at[way, step, r], send_sem.at[way, 0, r])
                landed[way, step, here] = (
                    landed[way, step, here].astype(F32) + own[home, here].astype(F32)
                ).astype(BF16)
            send(
                piece,
                landed.at[way, step - 1, here],
                send_sem.at[way, step - 1, r],
                recv_sem.at[way, step - 1, r],
                cut_device(way),
            )

    def reduce_last(own, landed, send_sem, recv_sem, here, r):
        total = own[c, here].astype(F32)
        for way in range(2):
            arrive(landed.at[way, 0, here], recv_sem.at[way, 0, r], send_sem.at[way, 0, r])
            total = total + landed[way, 0, here].astype(F32)
        return total

    def expert_reduce(step, r):
        reduce_event(part, part_in, red_send, red_recv, chunk_slots(r), step, r)

    loads[3].wait()
    loads[4].wait()
    for r in range(CHUNKS):
        gather_event(half_y, r)
        expert_chunk(r)
        expert_reduce(half_y, r)
        if r == 1:
            ring_next()
    for r in range(CHUNKS):
        expert_reduce(half_y - 1, r)
        if r in (0, 3):
            ring_next()
    for r in range(CHUNKS):
        expert_reduce(half_y - 2, r)
    while ring_events:
        ring_next()

    def dense_first(n):
        size = hidden // 4
        columns = pl.ds(n * size, size)
        dense_act[:, columns] = jax.nn.gelu(
            jnp.dot(
                norm[...],
                d_in[:, :, :, columns].reshape(width, size),
                preferred_element_type=F32,
            )
        ).astype(BF16)

    def dense_second(k):
        dense_part[k] = jnp.dot(
            dense_act[...],
            jnp.concatenate([d_out[k, 0], d_out[k, 1]], axis=1),
            preferred_element_type=F32,
        ).astype(BF16)

    for w in range(2):
        for place in range(n_chip):
            arrive(
                weights[w].at[chip(-place), 1 - core],
                sib_recv.at[w, place],
                sib_send.at[w, place],
            )
    steps = list(range(half_y - 3, 0, -1))
    for step in steps:
        for r in range(CHUNKS):
            expert_reduce(step, r)
            dense_first(r)

    def go_home(r):
        here = chunk_slots(r)
        result[here] = reduce_last(part, part_in, red_send, red_recv, here, r).astype(BF16)
        for slot in range(r * per_chunk, (r + 1) * per_chunk):
            if slot == 0:
                returned[e] = result[core]
                send(
                    result.at[1 - core],
                    returned.at[e],
                    ret_send.at[0],
                    ret_recv.at[e],
                    {"expert": sibling},
                )
            elif slot > 1:
                to = 2 * chip(offsets[slot // 2]) + slot % 2
                send(
                    result.at[slot], returned.at[e], ret_send.at[slot], ret_recv.at[e], {"expert": to}
                )

    def dense_slice(r):
        return pl.ds(r * drows, drows)

    def dense_reduce(step, r):
        reduce_event(dense_part, dense_part_in, dred_send, dred_recv, dense_slice(r), step, r)

    for k in range(n_cut):
        dense_second(k)
    for r in range(CHUNKS):
        dense_reduce(half_y, r)
    for r in range(CHUNKS):
        go_home(r)
    for step in range(half_y - 1, 0, -1):
        for r in range(CHUNKS):
            dense_reduce(step, r)

    for step in range(1, n_exp):
        sender = lax.rem(e + step, n_exp)
        arrive(returned.at[sender], ret_recv.at[sender], ret_send.at[0])
    expert_res = lax.dot_general(
        pick[...],
        returned[...].reshape(n_exp * cap, share),
        (((0,), (0,)), ((), ())),
        preferred_element_type=F32,
    )
    gate = jnp.transpose(jnp.broadcast_to(gate_ref[...], (128, rows)))[:, 0:1]
    dense_part_sum = tok[:, own_columns].astype(F32) + gate * expert_res
    for r in range(CHUNKS):
        here = dense_slice(r)
        total = reduce_last(dense_part, dense_part_in, dred_send, dred_recv, here, r)
        out_ref[here, :] = (
            dense_part_sum[r * drows : (r + 1) * drows] + total
        ).astype(BF16)

    for copy in started:
        copy.wait_send()


def local(tokens, route, gate_prob, norm_gain, dense_in, dense_out, expert_in, expert_out):
    n_exp = lax.axis_size("expert")
    n_cut = lax.axis_size("cuts")
    rows, width = tokens.shape
    share = width // n_cut
    hidden = expert_in.shape[2]
    cap = max(2, 3 * rows // (2 * n_exp))
    n_chip = n_exp // 2
    depth = dense_in.shape[0]
    half_y = n_cut // 2
    dims = (n_exp, n_cut, cap, rows, width, share, hidden)
    vmem = pl.BlockSpec(memory_space=pltpu.VMEM)
    hbm = pl.BlockSpec(memory_space=pl.ANY)
    dma = pltpu.SemaphoreType.DMA
    return pl.pallas_call(
        functools.partial(layer_kernel, dims),
        out_shape=jax.ShapeDtypeStruct((rows, share), BF16),
        in_specs=[hbm, vmem, vmem, vmem, hbm, hbm, hbm, hbm],
        out_specs=vmem,
        scratch_shapes=[
            pltpu.VMEM((rows, width), BF16),
            pltpu.VMEM((rows, width), BF16),
            pltpu.VMEM((n_exp * cap, rows), BF16),
            pltpu.VMEM((n_exp, cap, share), BF16),
            pltpu.VMEM((n_cut, n_exp, cap, share), BF16),
            pltpu.VMEM((width, hidden), BF16),
            pltpu.VMEM((hidden, width), BF16),
            pltpu.VMEM((n_chip, 2, depth, hidden), BF16),
            pltpu.VMEM((n_chip, 2, hidden, depth), BF16),
            pltpu.VMEM((n_exp // CHUNKS * cap, hidden), BF16),
            pltpu.VMEM((n_cut, n_exp, cap, share), BF16),
            pltpu.VMEM((2, half_y, n_exp, cap, share), BF16),
            pltpu.VMEM((n_exp, cap, share), BF16),
            pltpu.VMEM((n_exp, cap, share), BF16),
            pltpu.VMEM((rows, hidden), BF16),
            pltpu.VMEM((n_cut, rows, share), BF16),
            pltpu.VMEM((2, half_y, rows, share), BF16),
            dma((5,)),
            dma((n_exp,)),
            dma((n_exp,)),
            dma((2, half_y, CHUNKS)),
            dma((2, half_y, CHUNKS)),
            dma((2, 2, n_chip // 2)),
            dma((2, 2, n_chip // 2)),
            dma((2, n_chip)),
            dma((2, n_chip)),
            dma((2, half_y, CHUNKS)),
            dma((2, half_y, CHUNKS)),
            dma((n_exp,)),
            dma((n_exp,)),
            dma((2, half_y, CHUNKS)),
            dma((2, half_y, CHUNKS)),
        ],
        compiler_params=pltpu.CompilerParams(
            collective_id=0, has_side_effects=True, vmem_limit_bytes=60 * 1024 * 1024
        ),
        name="moe_layer",
    )(
        tokens,
        route.reshape(1, rows),
        gate_prob.reshape(1, rows),
        norm_gain.reshape(1, width),
        dense_in,
        dense_out,
        expert_in.reshape(width, hidden),
        expert_out.reshape(hidden, width),
    )


def solution(mesh):
    return jax.shard_map(
        local,
        mesh=mesh,
        in_specs=(
            P(("groups", "expert"), None),
            P(("groups", "expert"), None),
            P(("groups", "expert")),
            P(),
            P("expert", "cuts"),
            P("cuts", "expert"),
            P("expert", None, "cuts"),
            P("expert", "cuts", None),
        ),
        out_specs=P(("groups", "expert"), "cuts"),
        check_vma=False,
    )
```

time: 243 us -> 122 us (0.50)
  Pallas kernels: 0 us -> 119 us
  blocking collectives: 112 us -> 0 us
  waiting for transfers between devices: 67.9 us -> 0 us
  matrix products: 18.7 us -> 0 us
  between operations: 15 us -> 0.01 us
  other arithmetic: 13.1 us -> 0 us
  starting transfers between devices: 10.3 us -> 0 us
    pallas_call x0 -> x1, Pallas kernels: none -> 119 us  [local(): pl.pallas_call(functools.partial(layer_kernel, dims), out_shape=jax.Shape...]
    all_to_all x1 -> x0, blocking collectives: 112 us -> none  [local(): lax.all_to_all(outgoing, 'expert', split_axis=0, concat_axis=0, tiled=True)]
    all_gather x2 -> x0, waiting for transfers between devices: 27.8 us -> none  [the longest x1 27.8 us: residual_mlp(): lax.all_gather(dense_out, 'expert', axis=1, tiled=True)]
    reduce_scatter x2 -> x0, waiting for transfers between devices: 24.1 us -> none  [the longest x1 18.1 us: residual_mlp(): lax.psum_scatter(partial_out.astype(jnp.bfloat16), 'cuts', scatter_dimens...]
    dot_general x3 -> x0, matrix products: 18.7 us -> none  [the longest x1 9.92 us: residual_mlp(): jnp.dot(dense_act, lax.all_gather(dense_out, 'expert', axis=1, tiled=True...]
    all_to_all x1 -> x0, waiting for transfers between devices: 14.5 us -> none  [local(): lax.all_to_all(own_share, 'expert', split_axis=0, concat_axis=0, tiled=True)]
    all_to_all x1 -> x0, starting transfers between devices: 9.92 us -> none  [local(): lax.all_to_all(own_share, 'expert', split_axis=0, concat_axis=0, tiled=True)]
    scatter x1 -> x0, other arithmetic: 5.85 us -> none  [local(): jnp.zeros((experts * capacity, width), jnp.bfloat16).at[target].set(normed)]
  transfers between devices with their start and end apart: 5 -> 0, of which waited for: 4 -> 0; matrix products, arithmetic and copies ran while one was open for 13% -> 0% of each run, Pallas kernels for 0% -> 0%
where the time goes in v1:
time: 122 us; the launch traced here: 121 us
  Pallas kernels  119 us (98%)
  local copies, waits for them, and re-layouts  1.67 us (1%)
    pallas_call x1, Pallas kernels, local(): pl.pallas_call(functools.partial(layer_kernel, dims), out_shape=jax.Shape...  119 us

profile of v1, /device:TPU:513, one launch (start us, length us, event | category | flops | bytes accessed | tf_op | source)
XLA Modules:
  0.0 120.6 jit_solution(1751749551422033367)
XLA Ops:
  0.0 119.0 %moe_layer.1 = bf16[512,256]{1,0:T(8,128)(2,1)} custom-call(bf16[512,2048]{1,0:T(8,128)(2,1)} %tokens_hbm.1, s32[1,512]{1,0:T(1,128)} %bitcast.8, f32[1,512]{1,0:T(1,128)} %bitcast.9, f32[1,2048]{1,0:T(1,128)} %bitcast.7, bf16[128,1024]{1,0:T(8,128)(2,1)} %dense_in_hbm.1, bf16[1024,128]{1,0:T(8,128)(2,1)} %dense_out_hbm.1, bf16[2048,1024]{1,0:T(8,128)(2,1)} %bitcast.5, ...), custom_call_target="tpu_custom_call" | custom-call | tf_op jit(solution)/shard_map/moe_layer/pallas_call | solution.py:423
  119.0 1.7 %copy.10 = bf16[512,256]{1,0:T(8,128)(2,1)} copy(bf16[512,256]{1,0:T(8,128)(2,1)} %moe_layer.1) | data formatting | bytes 524288

commit v2 on v1

v2 whole, which is shorter than its diff:
```python
import functools

import jax
import jax.numpy as jnp
from jax import lax
from jax.experimental import pallas as pl
from jax.experimental.pallas import tpu as pltpu
from jax.sharding import PartitionSpec as P

MESH = pl.DeviceIdType.MESH
F32 = jnp.float32
BF16 = jnp.bfloat16
CHUNKS = 4


def layer_kernel(
    dims,
    tokens_hbm,
    route_ref,
    gate_ref,
    gain_ref,
    dense_in_hbm,
    dense_out_hbm,
    expert_in_hbm,
    expert_out_hbm,
    out_ref,
    tok,
    norm,
    pick,
    pick_home,
    gate_wide,
    outgoing,
    outgoing_near,
    arrived,
    w_in,
    w_out,
    d_in,
    d_out,
    inner,
    part,
    part_near,
    part_in,
    near,
    result,
    returned,
    dense_act,
    dense_part,
    dense_part_in,
    base,
    load_sem,
    near_send,
    near_recv,
    disp_send,
    disp_recv,
    gath_send,
    gath_recv,
    ring_send,
    ring_recv,
    sib_send,
    sib_recv,
    red_send,
    red_recv,
    ret_send,
    ret_recv,
    dred_send,
    dred_recv,
):
    n_exp, n_cut, cap, rows, width, share, hidden = dims
    n_chip = n_exp // 2
    half_x, half_y = n_chip // 2, n_cut // 2
    offsets = [0] + [(p + 1) // 2 if p % 2 else -(p // 2) for p in range(1, n_chip)]
    far = n_exp - 2
    size = -(-far // CHUNKS)
    size += size % 2
    chunks = [(first, min(size, n_exp - first)) for first in range(2, n_exp, size)]
    dsize = rows // CHUNKS
    dense_chunks = [(first, dsize) for first in range(0, rows, dsize)]

    e = lax.axis_index("expert")
    c = lax.axis_index("cuts")
    x = e // 2
    core = e - 2 * x
    other = 1 - core
    sibling = {"expert": 2 * x + other}

    def chip(offset):
        return lax.rem(x + offset + n_chip, n_chip)

    def cut(offset):
        return lax.rem(c + offset + n_cut, n_cut)

    def ring_device(way):
        return {"expert": 2 * chip(1 if way == 0 else -1) + core}

    def cut_device(way):
        return {"cuts": cut(1 if way == 0 else -1)}

    def remote(src, dst, send_sem, recv_sem, device):
        return pltpu.make_async_remote_copy(
            src_ref=src,
            dst_ref=dst,
            send_sem=send_sem,
            recv_sem=recv_sem,
            device_id=device,
            device_id_type=MESH,
        )

    def send(src, dst, send_sem, recv_sem, device):
        remote(src, dst, send_sem, recv_sem, device).start()

    def arrive(dst, recv_sem, send_sem):
        remote(dst, dst, send_sem, recv_sem, sibling).wait_recv()

    def sent(src, send_sem, recv_sem):
        remote(src, src, send_sem, recv_sem, sibling).wait_send()

    def halves(chunk):
        first, count = chunk
        return (
            pl.ds(first, count // 2),
            pl.ds(first + count // 2, count // 2),
        )

    loads = []
    for number, (src, dst) in enumerate(
        (
            (tokens_hbm, tok),
            (expert_in_hbm, w_in),
            (expert_out_hbm, w_out),
            (dense_in_hbm, d_in.at[x, core]),
            (dense_out_hbm, d_out.at[x, core]),
        )
    ):
        copy = pltpu.make_async_copy(src, dst, load_sem.at[number])
        copy.start()
        loads.append(copy)

    barrier = pltpu.get_barrier_semaphore()
    for step in range(1, n_exp):
        pl.semaphore_signal(
            barrier, inc=1, device_id={"expert": lax.rem(e + step, n_exp)}, device_id_type=MESH
        )
    for way in range(2):
        pl.semaphore_signal(barrier, inc=1, device_id=cut_device(way), device_id_type=MESH)

    route = route_ref[...]
    hot = lax.broadcasted_iota(jnp.int32, (n_exp, rows), 0) == route
    hot = jnp.where(hot, 1.0, 0.0).astype(F32)
    earlier = lax.broadcasted_iota(jnp.int32, (rows, rows), 0) < lax.broadcasted_iota(
        jnp.int32, (rows, rows), 1
    )
    earlier = jnp.where(earlier, 1.0, 0.0).astype(BF16)
    before = jnp.dot(hot.astype(BF16), earlier, preferred_element_type=F32)
    position = jnp.sum(before * hot, axis=0, keepdims=True)
    target = route * cap + position.astype(jnp.int32)
    slots = lax.broadcasted_iota(jnp.int32, (n_exp * cap, rows), 0)
    pick[...] = jnp.where(slots == target, 1.0, 0.0).astype(BF16)

    loads[0].wait()
    block = rows // 8

    @pl.loop(0, 8)
    def _(i):
        here = pl.ds(pl.multiple_of(i * block, block), block)
        wide = tok[here, :].astype(F32)
        meansq = jnp.mean(wide * wide, axis=-1, keepdims=True)
        norm[here, :] = (wide * lax.rsqrt(meansq + 1e-06) * gain_ref[...]).astype(BF16)

    own_columns = pl.ds(pl.multiple_of(c * share, share), share)
    outgoing[...] = (
        jnp.dot(pick[...], norm[:, own_columns], preferred_element_type=F32)
        .astype(BF16)
        .reshape(n_exp, cap, share)
    )
    pl.semaphore_wait(barrier, n_exp + 1)

    def chunk_of(slot):
        return (slot - 2) // size

    for p in range(1, n_chip):
        for k in range(2):
            to = 2 * chip(-offsets[p]) + k
            send(
                outgoing.at[to],
                arrived.at[c, 2 * p + core],
                disp_send,
                disp_recv.at[chunk_of(2 * p)],
                {"expert": to},
            )

    near_rows = pick[pl.ds(pl.multiple_of(2 * x * cap, 2 * cap), 2 * cap), :]
    for k in range(n_cut):
        outgoing_near[k] = (
            jnp.dot(near_rows, norm[:, pl.ds(k * share, share)], preferred_element_type=F32)
            .astype(BF16)
            .reshape(2, cap, share)
        )
    send(
        outgoing_near.at[:, other], arrived.at[:, core], near_send.at[0], near_recv.at[0], sibling
    )
    for k in range(n_cut):
        arrived[k, core] = outgoing_near[k, core]

    weights = (d_in, d_out)

    def ring_own(w):
        loads[3 + w].wait()
        own = weights[w].at[x, core]
        for way in range(2):
            send(own, own, ring_send.at[w], ring_recv.at[way, w, 0], ring_device(way))
        send(own, own, sib_send.at[w], sib_recv.at[w], sibling)

    def ring_event(w, hop):
        for way in range(2):
            if hop == half_x and w != way:
                continue
            origin = chip(-hop if way == 0 else hop)
            piece = weights[w].at[origin, core]
            arrive(piece, ring_recv.at[way, w, hop - 1], ring_send.at[w])
            if hop < half_x - 1 or (hop == half_x - 1 and w == way):
                send(piece, piece, ring_send.at[w], ring_recv.at[way, w, hop], ring_device(way))
            send(piece, piece, sib_send.at[w], sib_recv.at[w], sibling)

    ring_events = [(w, hop) for hop in range(1, half_x + 1) for w in range(2)]

    def ring_next():
        ring_event(*ring_events.pop(0))

    def gather_event(hop, r):
        first, count = chunks[r]
        whole = pl.ds(first, count)
        if hop == 0:
            arrive(arrived.at[c, whole], disp_recv.at[r], disp_send)
        for way in range(2):
            here = halves(chunks[r])[way] if hop == half_y else whole
            onward = halves(chunks[r])[way] if hop == half_y - 1 else here
            origin = cut(-hop if way == 0 else hop)
            if hop > 0:
                arrive(arrived.at[origin, here], gath_recv.at[way, hop - 1, r], gath_send)
            if hop < half_y:
                piece = arrived.at[origin, onward]
                send(piece, piece, gath_send, gath_recv.at[way, hop, r], cut_device(way))

    def expert_rows(first, count, keep):
        flat = jnp.concatenate(
            [
                arrived[k, pl.ds(first, count)].reshape(count * cap, share)
                for k in range(n_cut)
            ],
            axis=1,
        )
        for n in range(2):
            columns = pl.ds(n * (hidden // 2), hidden // 2)
            inner[pl.ds(0, count * cap), columns] = jax.nn.gelu(
                jnp.dot(flat, w_in[:, columns], preferred_element_type=F32)
            ).astype(BF16)
        for k in range(0, n_cut, 2):
            both = jnp.dot(
                inner[pl.ds(0, count * cap), :],
                w_out[:, pl.ds(k * share, 2 * share)],
                preferred_element_type=F32,
            ).astype(BF16)
            for j in range(2):
                keep(k + j, both[:, j * share : (j + 1) * share].reshape(count, cap, share))

    def expert_near():
        def keep(k, values):
            part_near[k] = values

        arrive(arrived.at[:, other], near_recv.at[0], near_send.at[0])
        expert_rows(0, 2, keep)
        send(
            part_near.at[:, other], near.at[:, core], near_send.at[1], near_recv.at[1], sibling
        )
        for k in range(n_cut):
            near[k, core] = part_near[k, core]

    def expert_chunk(r):
        first, count = chunks[r]

        def keep(k, values):
            part[k, pl.ds(first, count)] = values

        expert_rows(first, count, keep)

    def reduce_event(own, landed, send_sem, recv_sem, chunk, step, r):
        whole = pl.ds(*chunk)
        for way in range(2):
            half, rest = halves(chunk)[way], halves(chunk)[1 - way]
            home = cut(step if way == 0 else -step)
            to = step - 1
            if step == half_y:
                send(
                    own.at[home, half],
                    landed.at[way, to, half],
                    send_sem,
                    recv_sem.at[way, to, r],
                    cut_device(way),
                )
                continue
            here = half if step == half_y - 1 else whole
            arrive(landed.at[way, step, here], recv_sem.at[way, step, r], send_sem)
            landed[way, step, here] = (
                landed[way, step, here].astype(F32) + own[home, here].astype(F32)
            ).astype(BF16)
            if step == half_y - 1:
                landed[way, step, rest] = own[home, rest]
            send(
                landed.at[way, step, whole],
                landed.at[way, to, whole],
                send_sem,
                recv_sem.at[way, to, r],
                cut_device(way),
            )

    def reduce_last(own, landed, send_sem, recv_sem, chunk, r):
        whole = pl.ds(*chunk)
        total = own[c, whole].astype(F32)
        for way in range(2):
            arrive(landed.at[way, 0, whole], recv_sem.at[way, 0, r], send_sem)
            total = total + landed[way, 0, whole].astype(F32)
        return total

    def expert_reduce(step, r):
        reduce_event(part, part_in, red_send, red_recv, chunks[r], step, r)

    def go_home(r):
        first, count = chunks[r]
        result[pl.ds(first, count)] = reduce_last(
            part, part_in, red_send, red_recv, chunks[r], r
        ).astype(BF16)
        for slot in range(first, first + count):
            to = 2 * chip(offsets[slot // 2]) + slot % 2
            send(result.at[slot], returned.at[e], ret_send, ret_recv, {"expert": to})

    def dense_first(n):
        columns = pl.ds(n * (hidden // 2), hidden // 2)
        dense_act[:, columns] = jax.nn.gelu(
            jnp.dot(
                norm[...],
                d_in[:, :, :, columns].reshape(width, hidden // 2),
                preferred_element_type=F32,
            )
        ).astype(BF16)

    def dense_second(k):
        both = jnp.dot(
            dense_act[...],
            jnp.concatenate([d_out[k, 0], d_out[k, 1], d_out[k + 1, 0], d_out[k + 1, 1]], axis=1),
            preferred_element_type=F32,
        )
        rows_near = jnp.concatenate(
            [near[k].reshape(2 * cap, share), near[k + 1].reshape(2 * cap, share)], axis=1
        )
        both = both + gate_wide[:, 0:1] * jnp.dot(
            near_home, rows_near, preferred_element_type=F32
        )
        both = both.astype(BF16)
        dense_part[k] = both[:, :share]
        dense_part[k + 1] = both[:, share:]

    def dense_reduce(step, r):
        reduce_event(
            dense_part, dense_part_in, dred_send, dred_recv, dense_chunks[r], step, r
        )

    def home_tables():
        gate_wide[...] = jnp.transpose(jnp.broadcast_to(gate_ref[...], (128, rows)))
        wide = jnp.transpose(jnp.broadcast_to(target.astype(F32), (128, rows)))[:, 0:1]
        slot_of = lax.broadcasted_iota(jnp.int32, (rows, n_exp * cap), 1).astype(F32)
        pick_home[...] = jnp.where(slot_of == wide, 1.0, 0.0).astype(BF16)
        slot_of = lax.broadcasted_iota(jnp.int32, (rows, 2 * cap), 1) + 2 * x * cap
        return jnp.where(slot_of.astype(F32) == wide, 1.0, 0.0).astype(BF16)

    loads[1].wait()
    loads[2].wait()
    returned[pl.ds(2 * x, 2)] = jnp.zeros((2, cap, share), BF16)
    near_home = home_tables()
    expert_near()
    last = len(chunks) - 1
    gather_event(0, 0)
    gather_event(0, 1)
    ring_own(0)
    gather_event(0, 2)
    gather_event(0, 3)
    ring_own(1)
    for hop in range(1, half_y):
        for r in range(len(chunks)):
            gather_event(hop, r)
            if (hop, r) in ((1, 2), (2, 1), (2, 3)):
                ring_next()
    for r in range(len(chunks)):
        gather_event(half_y, r)
        expert_chunk(r)
        expert_reduce(half_y, r)
        if r in (0, 2):
            ring_next()
    for step in range(half_y - 1, 0, -1):
        for r in range(len(chunks)):
            expert_reduce(step, r)
            if (step, r) in ((3, 1), (3, 3), (2, 0)):
                ring_next()
            if (step, r) == (2, 1):
                arrive(d_in.at[:, other], sib_recv.at[0], sib_send.at[0])
                dense_first(0)
            if (step, r) == (2, 2):
                dense_first(1)
            if (step, r) == (2, 3):
                arrive(d_out.at[:, other], sib_recv.at[1], sib_send.at[1])
                arrive(near.at[:, other], near_recv.at[1], near_send.at[1])
            if step == 1:
                dense_second(2 * r)
    for r in range(CHUNKS):
        dense_reduce(half_y, r)
    for r in range(len(chunks)):
        go_home(r)
    for step in range(half_y - 1, 0, -1):
        for r in range(CHUNKS):
            dense_reduce(step, r)
            if (step, r) == (1, 0):
                arrive(returned.at[pl.ds(0, far)], ret_recv, ret_send)
                expert_res = jnp.dot(
                    pick_home[...],
                    returned[...].reshape(n_exp * cap, share),
                    preferred_element_type=F32,
                )
                base[...] = tok[:, own_columns].astype(F32) + gate_wide[:, 0:1] * expert_res
    for r in range(CHUNKS):
        here = pl.ds(*dense_chunks[r])
        total = reduce_last(dense_part, dense_part_in, dred_send, dred_recv, dense_chunks[r], r)
        out_ref[here, :] = (base[here, :] + total).astype(BF16)

    sent(outgoing.at[pl.ds(0, far)], disp_send, disp_recv.at[0])
    sent(outgoing_near.at[:, 0], near_send.at[0], near_recv.at[0])
    sent(part_near.at[:, 0], near_send.at[1], near_recv.at[1])
    sent(arrived.at[pl.ds(0, n_cut - 1), pl.ds(2, far)], gath_send, gath_recv.at[0, 0, 0])
    for w in range(2):
        sent(weights[w].at[pl.ds(0, n_chip - 1), 0], ring_send.at[w], ring_recv.at[0, w, 0])
        sent(weights[w].at[:, 0], sib_send.at[w], sib_recv.at[w])
    sent(part.at[pl.ds(0, n_cut - 1), pl.ds(2, far)], red_send, red_recv.at[0, 0, 0])
    sent(result.at[pl.ds(2, far)], ret_send, ret_recv)
    sent(dense_part.at[pl.ds(0, n_cut - 1)], dred_send, dred_recv.at[0, 0, 0])


def local(tokens, route, gate_prob, norm_gain, dense_in, dense_out, expert_in, expert_out):
    n_exp = lax.axis_size("expert")
    n_cut = lax.axis_size("cuts")
    rows, width = tokens.shape
    share = width // n_cut
    hidden = expert_in.shape[2]
    cap = max(2, 3 * rows // (2 * n_exp))
    n_chip = n_exp // 2
    depth = dense_in.shape[0]
    half_y = n_cut // 2
    dims = (n_exp, n_cut, cap, rows, width, share, hidden)
    vmem = pl.BlockSpec(memory_space=pltpu.VMEM)
    hbm = pl.BlockSpec(memory_space=pl.ANY)
    dma = pltpu.SemaphoreType.DMA
    return pl.pallas_call(
        functools.partial(layer_kernel, dims),
        out_shape=jax.ShapeDtypeStruct((rows, share), BF16),
        in_specs=[hbm, vmem, vmem, vmem, hbm, hbm, hbm, hbm],
        out_specs=vmem,
        scratch_shapes=[
            pltpu.VMEM((rows, width), BF16),
            pltpu.VMEM((rows, width), BF16),
            pltpu.VMEM((n_exp * cap, rows), BF16),
            pltpu.VMEM((rows, n_exp * cap), BF16),
            pltpu.VMEM((rows, 128), F32),
            pltpu.VMEM((n_exp, cap, share), BF16),
            pltpu.VMEM((n_cut, 2, cap, share), BF16),
            pltpu.VMEM((n_cut, n_exp, cap, share), BF16),
            pltpu.VMEM((width, hidden), BF16),
            pltpu.VMEM((hidden, width), BF16),
            pltpu.VMEM((n_chip, 2, depth, hidden), BF16),
            pltpu.VMEM((n_chip, 2, hidden, depth), BF16),
            pltpu.VMEM((-(-n_exp // CHUNKS) * cap, hidden), BF16),
            pltpu.VMEM((n_cut, n_exp, cap, share), BF16),
            pltpu.VMEM((n_cut, 2, cap, share), BF16),
            pltpu.VMEM((2, half_y, n_exp, cap, share), BF16),
            pltpu.VMEM((n_cut, 2, cap, share), BF16),
            pltpu.VMEM((n_exp, cap, share), BF16),
            pltpu.VMEM((n_exp, cap, share), BF16),
            pltpu.VMEM((rows, hidden), BF16),
            pltpu.VMEM((n_cut, rows, share), BF16),
            pltpu.VMEM((2, half_y, rows, share), BF16),
            pltpu.VMEM((rows, share), F32),
            dma((5,)),
            dma((2,)),
            dma((2,)),
            dma,
            dma((CHUNKS,)),
            dma,
            dma((2, half_y, CHUNKS)),
            dma((2,)),
            dma((2, 2, n_chip // 2)),
            dma((2,)),
            dma((2,)),
            dma,
            dma((2, half_y, CHUNKS)),
            dma,
            dma,
            dma,
            dma((2, half_y, CHUNKS)),
        ],
        compiler_params=pltpu.CompilerParams(
            collective_id=0, has_side_effects=True, vmem_limit_bytes=60 * 1024 * 1024
        ),
        name="moe_layer",
    )(
        tokens,
        route.reshape(1, rows),
        gate_prob.reshape(1, rows),
        norm_gain.reshape(1, width),
        dense_in,
        dense_out,
        expert_in.reshape(width, hidden),
        expert_out.reshape(hidden, width),
    )


def solution(mesh):
    return jax.shard_map(
        local,
        mesh=mesh,
        in_specs=(
            P(("groups", "expert"), None),
            P(("groups", "expert"), None),
            P(("groups", "expert")),
            P(),
            P("expert", "cuts"),
            P("cuts", "expert"),
            P("expert", None, "cuts"),
            P("expert", "cuts", None),
        ),
        out_specs=P(("groups", "expert"), "cuts"),
        check_vma=False,
    )
```

time: 122 us -> 111 us (0.910); the launches traced: 121 us -> 111 us
  Pallas kernels: 119 us -> 109 us
    pallas_call x1, Pallas kernels: 119 us -> 109 us  [local(): pl.pallas_call(functools.partial(layer_kernel, dims), out_shape=jax.Shape...]
where the time goes in v2:
time: 111 us
  Pallas kernels  109 us (98%)
  local copies, waits for them, and re-layouts  1.67 us (2%)
    pallas_call x1, Pallas kernels, local(): pl.pallas_call(functools.partial(layer_kernel, dims), out_shape=jax.Shape...  109 us

profile of v2, /device:TPU:513, one launch (start us, length us, event | category | flops | bytes accessed | tf_op | source)
XLA Modules:
  0.0 110.9 jit_solution(7106505335715392872)
XLA Ops:
  0.0 109.2 %moe_layer.1 = bf16[512,256]{1,0:T(8,128)(2,1)} custom-call(bf16[512,2048]{1,0:T(8,128)(2,1)} %tokens_hbm.1, s32[1,512]{1,0:T(1,128)} %bitcast.8, f32[1,512]{1,0:T(1,128)} %bitcast.9, f32[1,2048]{1,0:T(1,128)} %bitcast.7, bf16[128,1024]{1,0:T(8,128)(2,1)} %dense_in_hbm.1, bf16[1024,128]{1,0:T(8,128)(2,1)} %dense_out_hbm.1, bf16[2048,1024]{1,0:T(8,128)(2,1)} %bitcast.5, ...), custom_call_target="tpu_custom_call" | custom-call | tf_op jit(solution)/shard_map/moe_layer/pallas_call | solution.py:459
  109.2 1.7 %copy.10 = bf16[512,256]{1,0:T(8,128)(2,1)} copy(bf16[512,256]{1,0:T(8,128)(2,1)} %moe_layer.1) | data formatting | bytes 524288

commit v3 on v2

--- a/solution.py
+++ b/solution.py
@@ -11,6 +11,27 @@
 F32 = jnp.float32
 BF16 = jnp.bfloat16
 CHUNKS = 4
+
+
+ORDER = (
+    ("ring_own", 0), ("gather", 0, 0), ("gather", 0, 1), ("gather", 1, 0), ("gather", 0, 2),
+    ("gather", 1, 1), ("gather", 0, 3), ("ring", 0, 0, 1), ("gather", 2, 0), ("ring", 0, 1, 1),
+    ("gather", 1, 2), ("ring", 0, 0, 2), ("gather", 2, 1), ("gather", 1, 3), ("ring", 0, 1, 2),
+    ("ring_own", 1), ("gather", 3, 0), ("gather", 2, 2), ("ring", 0, 0, 3), ("gather", 3, 1),
+    ("ring", 0, 1, 3), ("gather", 2, 3), ("gather", 4, 0), ("expert", 0), ("ring", 1, 0, 1),
+    ("gather", 3, 2), ("gather", 4, 1), ("expert", 1), ("gather", 3, 3), ("ered", 4, 1),
+    ("gather", 4, 2), ("ring", 1, 1, 1), ("expert", 2), ("ring", 0, 0, 4), ("ring", 0, 1, 4),
+    ("ered", 4, 2), ("gather", 4, 3), ("expert", 3), ("ered", 3, 1), ("ring", 1, 0, 2),
+    ("ered", 4, 3), ("dfirst", 0), ("ered", 3, 2), ("ring", 1, 1, 2), ("dfirst", 1),
+    ("ered", 2, 1), ("ered", 3, 3), ("ring", 1, 0, 3), ("ered", 2, 2), ("ring", 1, 1, 3),
+    ("nrsend",), ("ered", 1, 1), ("ered", 2, 3), ("ring", 1, 0, 4), ("ered", 1, 2),
+    ("ring", 1, 1, 4), ("home", 1), ("ered", 1, 3), ("dsecond", 0), ("dred", 4, 0),
+    ("dred", 4, 1), ("dred", 4, 2), ("dred", 4, 3), ("home", 2), ("dsecond", 1), ("home", 3),
+    ("dred", 3, 0), ("dsecond", 2), ("dred", 3, 1), ("dred", 3, 2), ("dred", 3, 3),
+    ("dsecond", 3), ("dred", 2, 0), ("dred", 2, 1), ("base",), ("dred", 2, 2), ("dred", 2, 3),
+    ("dred", 1, 0), ("dred", 1, 1), ("dred", 1, 2), ("dred", 1, 3), ("last", 0), ("last", 1),
+    ("last", 2), ("last", 3),
+)
 
 
 def layer_kernel(
@@ -47,6 +68,7 @@
     dense_part,
     dense_part_in,
     base,
+    near_home,
     load_sem,
     near_send,
     near_recv,
@@ -64,6 +86,8 @@
     ret_recv,
     dred_send,
     dred_recv,
+    next_sem,
+    next_recv,
 ):
     n_exp, n_cut, cap, rows, width, share, hidden = dims
     n_chip = n_exp // 2
@@ -121,19 +145,19 @@
             pl.ds(first + count // 2, count // 2),
         )
 
-    loads = []
-    for number, (src, dst) in enumerate(
-        (
-            (tokens_hbm, tok),
-            (expert_in_hbm, w_in),
-            (expert_out_hbm, w_out),
-            (dense_in_hbm, d_in.at[x, core]),
-            (dense_out_hbm, d_out.at[x, core]),
-        )
-    ):
-        copy = pltpu.make_async_copy(src, dst, load_sem.at[number])
-        copy.start()
-        loads.append(copy)
+    loads = [
+        pltpu.make_async_copy(src, dst, load_sem.at[number])
+        for number, (src, dst) in enumerate(
+            (
+                (tokens_hbm, tok),
+                (expert_in_hbm, w_in),
+                (expert_out_hbm, w_out),
+                (dense_in_hbm, d_in.at[x, core]),
+                (dense_out_hbm, d_out.at[x, core]),
+            )
+        )
+    ]
+    loads[0].start()
 
     barrier = pltpu.get_barrier_semaphore()
     for step in range(1, n_exp):
@@ -157,6 +181,8 @@
     pick[...] = jnp.where(slots == target, 1.0, 0.0).astype(BF16)
 
     loads[0].wait()
+    for number in (3, 4, 1, 2):
+        loads[number].start()
     block = rows // 8
 
     @pl.loop(0, 8)
@@ -203,28 +229,28 @@
 
     weights = (d_in, d_out)
 
+    def ring_piece(w, origin, p):
+        half = weights[w].shape[2] // 2
+        return weights[w].at[origin, core, pl.ds(p * half, half)]
+
     def ring_own(w):
         loads[3 + w].wait()
+        for p in range(2):
+            piece = ring_piece(w, x, p)
+            for way in range(2):
+                send(piece, piece, ring_send.at[w], ring_recv.at[way, w, p, 0], ring_device(way))
         own = weights[w].at[x, core]
+        send(own, own, sib_send.at[w], sib_recv.at[w], sibling)
+
+    def ring_event(w, p, hop):
         for way in range(2):
-            send(own, own, ring_send.at[w], ring_recv.at[way, w, 0], ring_device(way))
-        send(own, own, sib_send.at[w], sib_recv.at[w], sibling)
-
-    def ring_event(w, hop):
-        for way in range(2):
-            if hop == half_x and w != way:
+            if hop == half_x and p != way:
                 continue
-            origin = chip(-hop if way == 0 else hop)
-            piece = weights[w].at[origin, core]
-            arrive(piece, ring_recv.at[way, w, hop - 1], ring_send.at[w])
-            if hop < half_x - 1 or (hop == half_x - 1 and w == way):
-                send(piece, piece, ring_send.at[w], ring_recv.at[way, w, hop], ring_device(way))
+            piece = ring_piece(w, chip(-hop if way == 0 else hop), p)
+            arrive(piece, ring_recv.at[way, w, p, hop - 1], ring_send.at[w])
+            if hop < half_x - 1 or (hop == half_x - 1 and p == way):
+                send(piece, piece, ring_send.at[w], ring_recv.at[way, w, p, hop], ring_device(way))
             send(piece, piece, sib_send.at[w], sib_recv.at[w], sibling)
-
-    ring_events = [(w, hop) for hop in range(1, half_x + 1) for w in range(2)]
-
-    def ring_next():
-        ring_event(*ring_events.pop(0))
 
     def gather_event(hop, r):
         first, count = chunks[r]
@@ -274,6 +300,24 @@
         )
         for k in range(n_cut):
             near[k, core] = part_near[k, core]
+
+    pairs = [(half_y, half_y - 1)]
+    pairs += [(-step, step - 1) for step in range(half_y - 1, 0, -1)]
+
+    def next_send():
+        for i, pair in enumerate(pairs):
+            for offset in pair:
+                k = cut(offset)
+                for slot in range(2, 6):
+                    to = 2 * chip(offsets[slot // 2]) + slot % 2
+                    place = slot // 2 * 2 + core
+                    send(
+                        part.at[k, slot],
+                        near.at[k, place],
+                        next_sem,
+                        next_recv.at[i],
+                        {"expert": to},
+                    )
 
     def expert_chunk(r):
         first, count = chunks[r]
@@ -334,6 +378,8 @@
             send(result.at[slot], returned.at[e], ret_send, ret_recv, {"expert": to})
 
     def dense_first(n):
+        if n == 0:
+            arrive(d_in.at[:, other], sib_recv.at[0], sib_send.at[0])
         columns = pl.ds(n * (hidden // 2), hidden // 2)
         dense_act[:, columns] = jax.nn.gelu(
             jnp.dot(
@@ -343,21 +389,24 @@
             )
         ).astype(BF16)
 
-    def dense_second(k):
+    def dense_second(i):
+        if i == 0:
+            arrive(d_out.at[:, other], sib_recv.at[1], sib_send.at[1])
+            arrive(near.at[:, other], near_recv.at[1], near_send.at[1])
+        arrive(near.at[pl.ds(0, 2), pl.ds(2, 4)], next_recv.at[i], next_sem)
+        ks = [cut(offset) for offset in pairs[i]]
         both = jnp.dot(
             dense_act[...],
-            jnp.concatenate([d_out[k, 0], d_out[k, 1], d_out[k + 1, 0], d_out[k + 1, 1]], axis=1),
+            jnp.concatenate([d_out[k, j] for k in ks for j in range(2)], axis=1),
             preferred_element_type=F32,
         )
-        rows_near = jnp.concatenate(
-            [near[k].reshape(2 * cap, share), near[k + 1].reshape(2 * cap, share)], axis=1
-        )
+        rows_near = jnp.concatenate([near[k].reshape(6 * cap, share) for k in ks], axis=1)
         both = both + gate_wide[:, 0:1] * jnp.dot(
-            near_home, rows_near, preferred_element_type=F32
+            near_home[...], rows_near, preferred_element_type=F32
         )
         both = both.astype(BF16)
-        dense_part[k] = both[:, :share]
-        dense_part[k + 1] = both[:, share:]
+        dense_part[ks[0]] = both[:, :share]
+        dense_part[ks[1]] = both[:, share:]
 
     def dense_reduce(step, r):
         reduce_event(
@@ -369,76 +418,66 @@
         wide = jnp.transpose(jnp.broadcast_to(target.astype(F32), (128, rows)))[:, 0:1]
         slot_of = lax.broadcasted_iota(jnp.int32, (rows, n_exp * cap), 1).astype(F32)
         pick_home[...] = jnp.where(slot_of == wide, 1.0, 0.0).astype(BF16)
-        slot_of = lax.broadcasted_iota(jnp.int32, (rows, 2 * cap), 1) + 2 * x * cap
-        return jnp.where(slot_of.astype(F32) == wide, 1.0, 0.0).astype(BF16)
-
-    loads[1].wait()
-    loads[2].wait()
-    returned[pl.ds(2 * x, 2)] = jnp.zeros((2, cap, share), BF16)
-    near_home = home_tables()
-    expert_near()
-    last = len(chunks) - 1
-    gather_event(0, 0)
-    gather_event(0, 1)
-    ring_own(0)
-    gather_event(0, 2)
-    gather_event(0, 3)
-    ring_own(1)
-    for hop in range(1, half_y):
-        for r in range(len(chunks)):
-            gather_event(hop, r)
-            if (hop, r) in ((1, 2), (2, 1), (2, 3)):
-                ring_next()
-    for r in range(len(chunks)):
-        gather_event(half_y, r)
-        expert_chunk(r)
-        expert_reduce(half_y, r)
-        if r in (0, 2):
-            ring_next()
-    for step in range(half_y - 1, 0, -1):
-        for r in range(len(chunks)):
-            expert_reduce(step, r)
-            if (step, r) in ((3, 1), (3, 3), (2, 0)):
-                ring_next()
-            if (step, r) == (2, 1):
-                arrive(d_in.at[:, other], sib_recv.at[0], sib_send.at[0])
-                dense_first(0)
-            if (step, r) == (2, 2):
-                dense_first(1)
-            if (step, r) == (2, 3):
-                arrive(d_out.at[:, other], sib_recv.at[1], sib_send.at[1])
-                arrive(near.at[:, other], near_recv.at[1], near_send.at[1])
-            if step == 1:
-                dense_second(2 * r)
-    for r in range(CHUNKS):
-        dense_reduce(half_y, r)
-    for r in range(len(chunks)):
-        go_home(r)
-    for step in range(half_y - 1, 0, -1):
-        for r in range(CHUNKS):
-            dense_reduce(step, r)
-            if (step, r) == (1, 0):
-                arrive(returned.at[pl.ds(0, far)], ret_recv, ret_send)
-                expert_res = jnp.dot(
-                    pick_home[...],
-                    returned[...].reshape(n_exp * cap, share),
-                    preferred_element_type=F32,
-                )
-                base[...] = tok[:, own_columns].astype(F32) + gate_wide[:, 0:1] * expert_res
-    for r in range(CHUNKS):
+        lane = lax.broadcasted_iota(jnp.int32, (rows, 6 * cap), 1)
+        first = jnp.where(
+            lane < 2 * cap,
+            2 * cap * x,
+            jnp.where(
+                lane < 4 * cap, 2 * cap * (chip(-1) - 1), 2 * cap * (chip(1) - 2)
+            ),
+        )
+        near_home[...] = jnp.where((lane + first).astype(F32) == wide, 1.0, 0.0).astype(BF16)
+
+    def dense_base():
+        arrive(returned.at[pl.ds(0, far - 4)], ret_recv, ret_send)
+        expert_res = jnp.dot(
+            pick_home[...],
+            returned[...].reshape(n_exp * cap, share),
+            preferred_element_type=F32,
+        )
+        base[...] = tok[:, own_columns].astype(F32) + gate_wide[:, 0:1] * expert_res
+
+    def dense_last(r):
         here = pl.ds(*dense_chunks[r])
         total = reduce_last(dense_part, dense_part_in, dred_send, dred_recv, dense_chunks[r], r)
         out_ref[here, :] = (base[here, :] + total).astype(BF16)
+
+    for offset in (-1, 0, 1):
+        returned[pl.ds(2 * chip(offset), 2)] = jnp.zeros((2, cap, share), BF16)
+
+    ring_own(0)
+    home_tables()
+    loads[1].wait()
+    loads[2].wait()
+    expert_near()
+    steps = {
+        "gather": gather_event,
+        "ring_own": ring_own,
+        "ring": ring_event,
+        "expert": expert_chunk,
+        "nrsend": next_send,
+        "ered": expert_reduce,
+        "home": go_home,
+        "dfirst": dense_first,
+        "dsecond": dense_second,
+        "dred": dense_reduce,
+        "base": dense_base,
+        "last": dense_last,
+    }
+    for name, *where in ORDER:
+        if (name, *where) != ("ring_own", 0):
+            steps[name](*where)
 
     sent(outgoing.at[pl.ds(0, far)], disp_send, disp_recv.at[0])
     sent(outgoing_near.at[:, 0], near_send.at[0], near_recv.at[0])
     sent(part_near.at[:, 0], near_send.at[1], near_recv.at[1])
     sent(arrived.at[pl.ds(0, n_cut - 1), pl.ds(2, far)], gath_send, gath_recv.at[0, 0, 0])
     for w in range(2):
-        sent(weights[w].at[pl.ds(0, n_chip - 1), 0], ring_send.at[w], ring_recv.at[0, w, 0])
+        sent(weights[w].at[pl.ds(0, n_chip - 1), 0], ring_send.at[w], ring_recv.at[0, w, 0, 0])
         sent(weights[w].at[:, 0], sib_send.at[w], sib_recv.at[w])
-    sent(part.at[pl.ds(0, n_cut - 1), pl.ds(2, far)], red_send, red_recv.at[0, 0, 0])
-    sent(result.at[pl.ds(2, far)], ret_send, ret_recv)
+    sent(part.at[:, pl.ds(2, 4)], next_sem, next_recv.at[0])
+    sent(part.at[pl.ds(0, n_cut - 1), pl.ds(6, far - 4)], red_send, red_recv.at[0, 0, 0])
+    sent(result.at[pl.ds(6, far - 4)], ret_send, ret_recv)
     sent(dense_part.at[pl.ds(0, n_cut - 1)], dred_send, dred_recv.at[0, 0, 0])
 
 
@@ -454,7 +493,7 @@
     half_y = n_cut // 2
     dims = (n_exp, n_cut, cap, rows, width, share, hidden)
     vmem = pl.BlockSpec(memory_space=pltpu.VMEM)
-    hbm = pl.BlockSpec(memory_space=pl.ANY)
+    hbm = pl.BlockSpec(memory_space=pltpu.HBM)
     dma = pltpu.SemaphoreType.DMA
     return pl.pallas_call(
         functools.partial(layer_kernel, dims),
@@ -478,13 +517,14 @@
             pltpu.VMEM((n_cut, n_exp, cap, share), BF16),
             pltpu.VMEM((n_cut, 2, cap, share), BF16),
             pltpu.VMEM((2, half_y, n_exp, cap, share), BF16),
-            pltpu.VMEM((n_cut, 2, cap, share), BF16),
+            pltpu.VMEM((n_cut, 6, cap, share), BF16),
             pltpu.VMEM((n_exp, cap, share), BF16),
             pltpu.VMEM((n_exp, cap, share), BF16),
             pltpu.VMEM((rows, hidden), BF16),
             pltpu.VMEM((n_cut, rows, share), BF16),
             pltpu.VMEM((2, half_y, rows, share), BF16),
             pltpu.VMEM((rows, share), F32),
+            pltpu.VMEM((rows, 6 * cap), BF16),
             dma((5,)),
             dma((2,)),
             dma((2,)),
@@ -493,7 +533,7 @@
             dma,
             dma((2, half_y, CHUNKS)),
             dma((2,)),
-            dma((2, 2, n_chip // 2)),
+            dma((2, 2, 2, n_chip // 2)),
             dma((2,)),
             dma((2,)),
             dma,
@@ -502,20 +542,27 @@
             dma,
             dma,
             dma((2, half_y, CHUNKS)),
+            dma,
+            dma((half_y,)),
         ],
         compiler_params=pltpu.CompilerParams(
-            collective_id=0, has_side_effects=True, vmem_limit_bytes=60 * 1024 * 1024
+            collective_id=0, has_side_effects=True, vmem_limit_bytes=52 * 1024 * 1024
         ),
         name="moe_layer",
     )(
-        tokens,
-        route.reshape(1, rows),
-        gate_prob.reshape(1, rows),
-        norm_gain.reshape(1, width),
-        dense_in,
-        dense_out,
-        expert_in.reshape(width, hidden),
-        expert_out.reshape(hidden, width),
+        *(
+            pltpu.with_memory_space_constraint(operand, pltpu.HBM)
+            for operand in (
+                tokens,
+                route.reshape(1, rows),
+                gate_prob.reshape(1, rows),
+                norm_gain.reshape(1, width),
+                dense_in,
+                dense_out,
+                expert_in.reshape(width, hidden),
+                expert_out.reshape(hidden, width),
+            )
+        )
     )
 
 

time: 111 us -> 104 us (0.937)
  Pallas kernels: 109 us -> 103 us
    pallas_call x1, Pallas kernels: 109 us -> 103 us  [local(): pl.pallas_call(functools.partial(layer_kernel, dims), out_shape=jax.Shape...]
where the time goes in v3:
time: 104 us
  Pallas kernels  103 us (99%)
    pallas_call x1, Pallas kernels, local(): pl.pallas_call(functools.partial(layer_kernel, dims), out_shape=jax.Shape...  103 us

profile of v3, /device:TPU:513, one launch (start us, length us, event | category | flops | bytes accessed | tf_op | source)
XLA Modules:
  0.0 104.1 jit_solution(10940976083623324647)
XLA Ops:
  0.0 103.4 %moe_layer.1 = bf16[512,256]{1,0:T(8,128)(2,1)S(1)} custom-call(bf16[512,2048]{1,0:T(8,128)(2,1)} %tokens_hbm.1, s32[1,512]{1,0:T(1,128)} %bitcast.8, f32[1,512]{1,0:T(1,128)} %bitcast.9, f32[1,2048]{1,0:T(1,128)} %bitcast.7, bf16[128,1024]{1,0:T(8,128)(2,1)} %dense_in_hbm.1, bf16[1024,128]{1,0:T(8,128)(2,1)} %dense_out_hbm.1, bf16[2048,1024]{1,0:T(8,128)(2,1)} %bitcast.5, ...), custom_call_target="tpu_custom_call" | custom-call | tf_op jit(solution)/shard_map/moe_layer/pallas_call | solution.py:498
  103.4 0.7 copy.10

commit v4 on v3

--- a/solution.py
+++ b/solution.py
@@ -11,6 +11,7 @@
 F32 = jnp.float32
 BF16 = jnp.bfloat16
 CHUNKS = 4
+BLOCKS = 4
 
 
 ORDER = (
@@ -37,14 +38,18 @@
 def layer_kernel(
     dims,
     tokens_hbm,
-    route_ref,
-    gate_ref,
-    gain_ref,
+    route_hbm,
+    gate_hbm,
+    gain_hbm,
     dense_in_hbm,
     dense_out_hbm,
     expert_in_hbm,
     expert_out_hbm,
     out_ref,
+    route_ref,
+    gate_ref,
+    gain_ref,
+    scale,
     tok,
     norm,
     pick,
@@ -145,19 +150,24 @@
             pl.ds(first + count // 2, count // 2),
         )
 
+    block = rows // BLOCKS
+    blocks = [pl.ds(n * block, block) for n in range(BLOCKS)]
+    copies = [
+        (expert_in_hbm, w_in),
+        (expert_out_hbm, w_out),
+        (dense_in_hbm, d_in.at[x, core]),
+        (dense_out_hbm, d_out.at[x, core]),
+        (route_hbm, route_ref),
+        (gain_hbm, gain_ref),
+        (gate_hbm, gate_ref),
+    ]
+    copies += [(tokens_hbm.at[here], tok.at[here]) for here in blocks]
     loads = [
         pltpu.make_async_copy(src, dst, load_sem.at[number])
-        for number, (src, dst) in enumerate(
-            (
-                (tokens_hbm, tok),
-                (expert_in_hbm, w_in),
-                (expert_out_hbm, w_out),
-                (dense_in_hbm, d_in.at[x, core]),
-                (dense_out_hbm, d_out.at[x, core]),
-            )
-        )
+        for number, (src, dst) in enumerate(copies)
     ]
-    loads[0].start()
+    for copy in loads[4:]:
+        copy.start()
 
     barrier = pltpu.get_barrier_semaphore()
     for step in range(1, n_exp):
@@ -167,6 +177,7 @@
     for way in range(2):
         pl.semaphore_signal(barrier, inc=1, device_id=cut_device(way), device_id_type=MESH)
 
+    loads[4].wait()
     route = route_ref[...]
     hot = lax.broadcasted_iota(jnp.int32, (n_exp, rows), 0) == route
     hot = jnp.where(hot, 1.0, 0.0).astype(F32)
@@ -180,19 +191,18 @@
     slots = lax.broadcasted_iota(jnp.int32, (n_exp * cap, rows), 0)
     pick[...] = jnp.where(slots == target, 1.0, 0.0).astype(BF16)
 
-    loads[0].wait()
-    for number in (3, 4, 1, 2):
+    own_columns = pl.ds(pl.multiple_of(c * share, share), share)
+    loads[5].wait()
+    for n, here in enumerate(blocks):
+        loads[7 + n].wait()
+        wide = tok[here, :].astype(F32)
+        factor = lax.rsqrt(jnp.mean(wide * wide, axis=-1, keepdims=True) + 1e-06)
+        scale[here, :] = jnp.broadcast_to(factor, (block, 128))
+        norm[here, own_columns] = (
+            tok[here, own_columns].astype(F32) * factor * gain_ref[:, own_columns]
+        ).astype(BF16)
+    for number in (2, 3, 0, 1):
         loads[number].start()
-    block = rows // 8
-
-    @pl.loop(0, 8)
-    def _(i):
-        here = pl.ds(pl.multiple_of(i * block, block), block)
-        wide = tok[here, :].astype(F32)
-        meansq = jnp.mean(wide * wide, axis=-1, keepdims=True)
-        norm[here, :] = (wide * lax.rsqrt(meansq + 1e-06) * gain_ref[...]).astype(BF16)
-
-    own_columns = pl.ds(pl.multiple_of(c * share, share), share)
     outgoing[...] = (
         jnp.dot(pick[...], norm[:, own_columns], preferred_element_type=F32)
         .astype(BF16)
@@ -214,6 +224,12 @@
                 {"expert": to},
             )
 
+    @pl.loop(0, 8)
+    def _(n):
+        here = pl.ds(pl.multiple_of(n * (rows // 8), rows // 8), rows // 8)
+        wide = tok[here, :].astype(F32)
+        norm[here, :] = (wide * scale[here, 0:1] * gain_ref[...]).astype(BF16)
+
     near_rows = pick[pl.ds(pl.multiple_of(2 * x * cap, 2 * cap), 2 * cap), :]
     for k in range(n_cut):
         outgoing_near[k] = (
@@ -234,7 +250,7 @@
         return weights[w].at[origin, core, pl.ds(p * half, half)]
 
     def ring_own(w):
-        loads[3 + w].wait()
+        loads[2 + w].wait()
         for p in range(2):
             piece = ring_piece(w, x, p)
             for way in range(2):
@@ -446,9 +462,10 @@
         returned[pl.ds(2 * chip(offset), 2)] = jnp.zeros((2, cap, share), BF16)
 
     ring_own(0)
+    loads[6].wait()
     home_tables()
+    loads[0].wait()
     loads[1].wait()
-    loads[2].wait()
     expert_near()
     steps = {
         "gather": gather_event,
@@ -498,9 +515,13 @@
     return pl.pallas_call(
         functools.partial(layer_kernel, dims),
         out_shape=jax.ShapeDtypeStruct((rows, share), BF16),
-        in_specs=[hbm, vmem, vmem, vmem, hbm, hbm, hbm, hbm],
+        in_specs=[hbm] * 8,
         out_specs=vmem,
         scratch_shapes=[
+            pltpu.VMEM((1, rows), jnp.int32),
+            pltpu.VMEM((1, rows), F32),
+            pltpu.VMEM((1, width), F32),
+            pltpu.VMEM((rows, 128), F32),
             pltpu.VMEM((rows, width), BF16),
             pltpu.VMEM((rows, width), BF16),
             pltpu.VMEM((n_exp * cap, rows), BF16),
@@ -525,7 +546,7 @@
             pltpu.VMEM((2, half_y, rows, share), BF16),
             pltpu.VMEM((rows, share), F32),
             pltpu.VMEM((rows, 6 * cap), BF16),
-            dma((5,)),
+            dma((7 + BLOCKS,)),
             dma((2,)),
             dma((2,)),
             dma,

time: 104 us -> 103 us (level); the launches traced: 104 us -> 101 us
  Pallas kernels: 103 us -> 101 us
    pallas_call x1, Pallas kernels: 103 us -> 101 us  [local(): pl.pallas_call(functools.partial(layer_kernel, dims), out_shape=jax.Shape...]
where the time goes in v4:
time: 103 us; the launch traced here: 101 us
  Pallas kernels  101 us (98%)
    pallas_call x1, Pallas kernels, local(): pl.pallas_call(functools.partial(layer_kernel, dims), out_shape=jax.Shape...  101 us

profile of v4, /device:TPU:513, one launch (start us, length us, event | category | flops | bytes accessed | tf_op | source)
XLA Modules:
  0.0 101.4 jit_solution(16567034049295486769)
XLA Ops:
  0.0 100.7 %moe_layer.1 = bf16[512,256]{1,0:T(8,128)(2,1)S(1)} custom-call(bf16[512,2048]{1,0:T(8,128)(2,1)} %tokens_hbm.1, s32[1,512]{1,0:T(1,128)} %bitcast.8, f32[1,512]{1,0:T(1,128)} %bitcast.9, f32[1,2048]{1,0:T(1,128)} %bitcast.7, bf16[128,1024]{1,0:T(8,128)(2,1)} %dense_in_hbm.1, bf16[1024,128]{1,0:T(8,128)(2,1)} %dense_out_hbm.1, bf16[2048,1024]{1,0:T(8,128)(2,1)} %bitcast.5, ...), custom_call_target="tpu_custom_call" | custom-call | tf_op jit(solution)/shard_map/moe_layer/pallas_call | solution.py:515
  100.7 0.7 copy.10

commit v5 on v4

--- a/solution.py
+++ b/solution.py
@@ -23,15 +23,15 @@
     ("gather", 3, 2), ("gather", 4, 1), ("expert", 1), ("gather", 3, 3), ("ered", 4, 1),
     ("gather", 4, 2), ("ring", 1, 1, 1), ("expert", 2), ("ring", 0, 0, 4), ("ring", 0, 1, 4),
     ("ered", 4, 2), ("gather", 4, 3), ("expert", 3), ("ered", 3, 1), ("ring", 1, 0, 2),
-    ("ered", 4, 3), ("dfirst", 0), ("ered", 3, 2), ("ring", 1, 1, 2), ("dfirst", 1),
-    ("ered", 2, 1), ("ered", 3, 3), ("ring", 1, 0, 3), ("ered", 2, 2), ("ring", 1, 1, 3),
-    ("nrsend",), ("ered", 1, 1), ("ered", 2, 3), ("ring", 1, 0, 4), ("ered", 1, 2),
-    ("ring", 1, 1, 4), ("home", 1), ("ered", 1, 3), ("dsecond", 0), ("dred", 4, 0),
-    ("dred", 4, 1), ("dred", 4, 2), ("dred", 4, 3), ("home", 2), ("dsecond", 1), ("home", 3),
-    ("dred", 3, 0), ("dsecond", 2), ("dred", 3, 1), ("dred", 3, 2), ("dred", 3, 3),
-    ("dsecond", 3), ("dred", 2, 0), ("dred", 2, 1), ("base",), ("dred", 2, 2), ("dred", 2, 3),
-    ("dred", 1, 0), ("dred", 1, 1), ("dred", 1, 2), ("dred", 1, 3), ("last", 0), ("last", 1),
-    ("last", 2), ("last", 3),
+    ("ered", 4, 3), ("dfirst", 0), ("ered", 3, 2), ("ring", 1, 1, 2), ("nrsend", 0),
+    ("dfirst", 1), ("ered", 2, 1), ("ered", 3, 3), ("ring", 1, 0, 3), ("ered", 2, 2),
+    ("ring", 1, 1, 3), ("nrsend", 1), ("nrsend", 2), ("nrsend", 3), ("ered", 1, 1),
+    ("ered", 2, 3), ("ring", 1, 0, 4), ("ered", 1, 2), ("ring", 1, 1, 4), ("ered", 1, 3),
+    ("dsecond", 0), ("dred", 4, 0), ("dred", 4, 1), ("dred", 4, 2), ("dred", 4, 3), ("home", 1),
+    ("home", 2), ("dsecond", 1), ("home", 3), ("dred", 3, 0), ("dsecond", 2), ("dred", 3, 1),
+    ("dred", 3, 2), ("dred", 3, 3), ("dsecond", 3), ("dred", 2, 0), ("dred", 2, 1),
+    ("dred", 2, 2), ("dred", 2, 3), ("dred", 1, 0), ("dred", 1, 1), ("base",), ("dred", 1, 2),
+    ("dred", 1, 3), ("last", 0), ("last", 1), ("last", 2), ("last", 3),
 )
 
 
@@ -320,20 +320,17 @@
     pairs = [(half_y, half_y - 1)]
     pairs += [(-step, step - 1) for step in range(half_y - 1, 0, -1)]
 
-    def next_send():
-        for i, pair in enumerate(pairs):
-            for offset in pair:
-                k = cut(offset)
-                for slot in range(2, 6):
-                    to = 2 * chip(offsets[slot // 2]) + slot % 2
-                    place = slot // 2 * 2 + core
-                    send(
-                        part.at[k, slot],
-                        near.at[k, place],
-                        next_sem,
-                        next_recv.at[i],
-                        {"expert": to},
-                    )
+    def next_send(i):
+        for offset in pairs[i]:
+            k = cut(offset)
+            for slot in range(2, 6):
+                send(
+                    part.at[k, slot],
+                    near.at[k, slot // 2 * 2 + core],
+                    next_sem,
+                    next_recv.at[i],
+                    {"expert": 2 * chip(offsets[slot // 2]) + slot % 2},
+                )
 
     def expert_chunk(r):
         first, count = chunks[r]

time: 103 us -> 101 us (0.981); the launches traced: 101 us -> 101 us
  no operation moved by 1% of the time
where the time goes in v5:
time: 101 us
  Pallas kernels  100 us (99%)
    pallas_call x1, Pallas kernels, local(): pl.pallas_call(functools.partial(layer_kernel, dims), out_shape=jax.Shape...  100 us

profile of v5, /device:TPU:513, one launch (start us, length us, event | category | flops | bytes accessed | tf_op | source)
XLA Modules:
  0.0 101.2 jit_solution(18117842572947475205)
XLA Ops:
  0.0 100.5 %moe_layer.1 = bf16[512,256]{1,0:T(8,128)(2,1)S(1)} custom-call(bf16[512,2048]{1,0:T(8,128)(2,1)} %tokens_hbm.1, s32[1,512]{1,0:T(1,128)} %bitcast.8, f32[1,512]{1,0:T(1,128)} %bitcast.9, f32[1,2048]{1,0:T(1,128)} %bitcast.7, bf16[128,1024]{1,0:T(8,128)(2,1)} %dense_in_hbm.1, bf16[1024,128]{1,0:T(8,128)(2,1)} %dense_out_hbm.1, bf16[2048,1024]{1,0:T(8,128)(2,1)} %bitcast.5, ...), custom_call_target="tpu_custom_call" | custom-call | tf_op jit(solution)/shard_map/moe_layer/pallas_call | solution.py:512
  100.5 0.7 copy.10
